TPU v7x, 32 devices: a whole 2x2x4 slice. The times are simulated.
32 devices in a mesh: band: 16 (over z, y, core), spin: 2 (over x).
Axes of the slice: x: 2, y: 2, z: 4, core: 2. Of those that a mesh axis runs over, the one named last changes fastest.
Arguments:
- coefficients: bfloat16 [2, 2, 32, 524288], P('spin', None, 'band'), may hold values from -1 to 1
- occupation: int32 [2, 32], P('spin', 'band'), may hold values from 0 to 1000
- miller: int32 [3, 524288], P(None, ('band', 'spin')), may hold values from -8 to 8
- density: float32 [2, 256, 128, 128], P('spin', 'band'), may hold values from 0.25 to 2
- local_factor: float32 [2, 256, 128, 128], P(None, None, 'band'), may hold values from -1.2 to 1.2
Outputs:
- stress: float32 [6], replicated
- kinetic_density: float32 [524288], P(('band', 'spin'))
- gradient_square: float32 [2, 256, 128, 128], P('spin', 'band')
All inputs are finite; a program needn't handle non-finite values.
Results may differ from a plain program's by a relative error of at most 0.0003.
Values sent between devices are 32-bit elements; how exact they have to be, the bound alone decides.
No kernel may reach another device: no remote copies, remote signals or barrier semaphores. Data moves between devices by JAX's collectives and lax.ppermute only.
A program may use at most 64 MiB of HBM per device.

v0:
```python
import numpy as np
import jax
import jax.numpy as jnp
from jax import lax
from jax.sharding import PartitionSpec as P

occupation_unit = 1000.0
kpoint = (0.25, 0.125, 0.375)
spacing = 0.25
HIGH = lax.Precision.HIGH


def derivative_table(length):
    wrapped = np.mod(np.arange(length)[:, None] - np.arange(length)[None, :], length)
    angles = np.pi / length * wrapped
    sines = np.where(wrapped == 0, 1.0, np.sin(angles))
    parity = 1.0 - 2.0 * (wrapped % 2)
    return np.where(wrapped == 0, 0.0, 0.5 * parity * np.cos(angles) / sines).astype(np.float32)


def fourier_tables(length):
    phases = np.mod(np.arange(length)[:, None] * np.arange(length)[None, :], length) * (
        2.0 * np.pi / length
    )
    return (np.cos(phases), np.sin(phases))


def frequencies(length):
    positions = np.arange(length)
    signed = np.where(positions >= length // 2, positions - length, positions)
    return (2.0 * np.pi / length * signed).astype(np.float32)


def halves(values, axis, mine):
    return (
        lax.dynamic_index_in_dim(values, mine, axis, keepdims=False),
        lax.dynamic_index_in_dim(values, 1 - mine, axis, keepdims=False),
    )


def pair_up(size, bit):
    return [(i, i ^ bit) for i in range(size)]


def scatter_sum(values, band_devices, band, spin):
    tail = values.shape[2:]
    spins = values.shape[1]
    bit = 1
    left = band_devices
    done_spin = False
    rest = values.reshape((left, spins) + tail)
    while left > 1:
        mine = band // bit % 2
        rest = rest.reshape((left // 2, 2) + rest.shape[1:])
        keep, give = halves(rest, 1, mine)
        rest = keep + lax.ppermute(give, "band", pair_up(band_devices, bit))
        left //= 2
        bit *= 2
        if not done_spin:
            keep, give = halves(rest, 1, spin)
            rest = keep + lax.ppermute(give, "spin", pair_up(spins, 1))
            done_spin = True
    return rest.reshape(tail)


def shards(coefficients, occupation, miller, density, local_factor):
    band_devices = lax.axis_size("band")
    spins = lax.axis_size("spin")
    band = lax.axis_index("band")
    spin = lax.axis_index("spin")
    planes, nx, ny = density.shape[1:]
    nz = planes * band_devices
    rows = nx // band_devices
    cell_count = nz * nx * ny
    waves = coefficients.shape[3]
    dens = density[0]
    dens_send = dens.reshape(planes, band_devices, rows, ny).transpose(1, 0, 2, 3)
    dens_col = lax.all_to_all(dens_send, "band", 0, 0, tiled=True).reshape(nz, rows * ny)
    share = planes // spins
    keep, give = halves(dens.reshape(spins, share, nx, ny), 0, spin)
    total = keep + lax.ppermute(give, "spin", pair_up(spins, 1))
    weights = occupation[0].astype(jnp.float32) / occupation_unit
    piece = coefficients[0].astype(jnp.float32)
    partial = jnp.sum((piece[0] * piece[0] + piece[1] * piece[1]) * weights[:, None], axis=0)
    chunk = waves // (band_devices * spins)
    kinetic_weight = scatter_sum(
        partial.reshape(band_devices, spins, chunk // 128, 128), band_devices, band, spin
    )
    cos_x, sin_x = fourier_tables(nx)
    cos_y, sin_y = fourier_tables(ny)
    cos_z, sin_z = fourier_tables(nz)
    part = ny // spins
    table_y = np.stack(
        [
            np.stack(
                [
                    np.concatenate([cos_y[:, p : p + part], -sin_y[:, p : p + part]], 1),
                    np.concatenate([-sin_y[:, p : p + part], -cos_y[:, p : p + part]], 1),
                ]
            )
            for p in range(0, ny, part)
        ]
    ).astype(np.float32)
    along = jnp.einsum("zxj,pcjm->pczxm", total, table_y, precision=HIGH)
    table_x = np.stack([cos_x, sin_x]).reshape(2, band_devices, rows, nx).astype(np.float32)
    plane = jnp.einsum("cbrj,pczjm->bpzrm", table_x, along, precision=HIGH)
    lanes = plane.shape[-1]
    plane = plane.reshape(band_devices * spins, share, rows, lanes)
    column = lax.all_to_all(plane, ("band", "spin"), 0, 0, tiled=True).reshape(nz, rows * lanes)
    gradz_col = jnp.dot(derivative_table(nz), dens_col, precision=HIGH)
    gradz_back = lax.all_to_all(
        gradz_col.reshape(band_devices, planes, rows, ny), "band", 0, 0, tiled=True
    )
    grad_z = gradz_back.transpose(1, 0, 2, 3).reshape(planes, nx, ny)
    first = jnp.dot((cos_z / cell_count).astype(np.float32), column, precision=HIGH).reshape(
        nz, rows, lanes
    )
    second = jnp.dot((sin_z / cell_count).astype(np.float32), column, precision=HIGH).reshape(
        nz, rows, lanes
    )
    spectrum = first + jnp.concatenate([second[..., part:], -second[..., :part]], axis=-1)
    factor = lax.dynamic_slice_in_dim(local_factor, spin * part, part, 3)
    factor = jnp.concatenate([factor[0], factor[1]], axis=-1)
    freq_z = jnp.asarray(frequencies(nz))[:, None, None]
    freq_x = lax.dynamic_slice_in_dim(jnp.asarray(frequencies(nx)), band * rows, rows, 0)[:, None]
    freq_y = lax.dynamic_slice_in_dim(jnp.asarray(frequencies(ny)), spin * part, part, 0)
    freq_y = jnp.concatenate([freq_y, freq_y])[None, :]
    length_sq = freq_x * freq_x + freq_y * freq_y + freq_z * freq_z
    positive = length_sq > 0
    inverse = jnp.where(positive, 1.0 / jnp.where(positive, length_sq, 1.0), 0.0)
    hartree = 4.0 * np.pi * spectrum * spectrum * inverse
    both = 2.0 * (hartree * inverse + spectrum * factor)
    trace = jnp.sum(hartree, axis=0)
    sum_0 = jnp.sum(both, axis=0)
    sum_1 = jnp.sum(both * freq_z, axis=0)
    sum_2 = jnp.sum(both * (freq_z * freq_z), axis=0)
    recip = [
        sum_0 * freq_x * freq_x - trace,
        sum_0 * freq_y * freq_y - trace,
        sum_2 - trace,
        sum_1 * freq_y,
        sum_1 * freq_x,
        sum_0 * freq_x * freq_y,
    ]
    recip = [jnp.sum(r, axis=0) for r in recip]
    deriv_x = derivative_table(nx)
    deriv_y = derivative_table(ny)
    grad_x = jnp.einsum("ik,zky->ziy", deriv_x, dens, precision=HIGH)
    grad_y = jnp.einsum("zxk,ik->zxi", dens, deriv_y, precision=HIGH)
    square = grad_x * grad_x + grad_y * grad_y + grad_z * grad_z
    kernel = dens ** (-1.0 / 3.0) / (1.0 + square / (4.0 * dens * dens + 1.0)) * (-1.0 / cell_count)

    def six(weighting, a, b, c, axes):
        wa, wb = (weighting * a, weighting * b)
        return [
            jnp.sum(v, axis=axes)
            for v in (wa * a, wb * b, weighting * c * c, wb * c, wa * c, wa * b)
        ]

    xc = six(kernel, grad_x, grad_y, grad_z, (0, 1))
    kvec = jnp.array(kpoint, jnp.float32)
    gvec = spacing * (
        miller.reshape(3, chunk // 128, 128).astype(jnp.float32) + kvec[:, None, None]
    )
    kinetic_density = 0.5 * (gvec[0] ** 2 + gvec[1] ** 2 + gvec[2] ** 2) * kinetic_weight
    kinetic = six(kinetic_weight * (-1.0 / waves), gvec[0], gvec[1], gvec[2], 0)
    lanewise = jnp.stack([r + x + k for r, x, k in zip(recip, xc, kinetic)])
    stress = jnp.sum(lax.psum(lanewise, ("band", "spin")), axis=1)
    return (stress, kinetic_density.reshape(chunk), square[None])


def solution(mesh):
    return jax.shard_map(
        shards,
        mesh=mesh,
        in_specs=(
            P("spin", None, "band", None),
            P("spin", "band"),
            P(None, ("band", "spin")),
            P("spin", "band", None, None),
            P(None, None, "band", None),
        ),
        out_specs=(P(), P(("band", "spin")), P("spin", "band", None, None)),
        check_vma=False,
    )
```

profile of v0, /device:TPU:0, one launch (start us, length us, event | category | flops | bytes accessed | tf_op | source)
XLA Modules:
  0.0 179.8 jit_solution(8025798165100008383)
XLA Ops:
  0.6 2.3 %copy_bitcast_fusion = f32[16,16,8,128]{3,2,1,0:T(8,128)} fusion(f32[1,16,128,128]{3,2,1,0:T(8,128)} %param.19), kind=kLoop, calls=%fused_computation.46 | loop fusion | bytes 2097152 | tf_op jit(solution)/shard_map/transpose | solution.py:77
  2.9 7.5 %all-to-all-start.1 = ((f32[16,16,8,128]{3,2,1,0:T(8,128)}), f32[16,16,8,128]{3,2,1,0:T(8,128)}, u32[]{:S(2)}, u32[]{:S(2)}) async-start(f32[16,16,8,128]{3,2,1,0:T(8,128)} %copy_bitcast_fusion), calls=%async_computation.1 | async-start | bytes 2097152 | tf_op jit(solution)/shard_map/all_to_all | solution.py:78
  10.4 6.6 %convert_element_type.18 = f32[1,2,2,524288]{3,2,1,0:T(2,128)} convert(bf16[1,2,2,524288]{3,2,1,0:T(2,128)(2,1)} %param.16) | non-fusion elementwise | flops 2097152 | bytes 12582912 | tf_op jit(solution)/shard_map/convert_element_type | solution.py:83
  17.1 23.5 %fusion.3 = f32[524288]{0:T(1024)S(1)} fusion(f32[1,2,2,524288]{3,2,1,0:T(2,128)} %convert_element_type.18, f32[2]{0:T(128)S(1)} %multiply_bitcast_fusion.1), kind=kLoop, calls=%fused_computation.5 | loop fusion | flops 4718592 | bytes 10485768 | tf_op jit(solution)/shard_map/reduce_sum | solution.py:84
  40.6 1.0 dynamic-slice_bitcast_fusion.2
  42.2 0.9 dynamic-slice_bitcast_fusion.4
  43.0 1.5 collective-permute-start
  45.6 1.4 bitcast_add_fusion
  47.0 0.8 dynamic-slice_bitcast_fusion.3
  48.4 9.7 %collective-permute-done = f32[8,128,128]{2,1,0:T(8,128)} collective-permute-done((f32[8,128,128]{2,1,0:T(8,128)}, f32[8,128,128]{2,1,0:T(8,128)}, u32[]{:S(2)}, u32[]{:S(2)}) %collective-permute-start) | collective-permute-done | bytes 524320 | tf_op jit(solution)/shard_map/ppermute | solution.py:81
  58.1 2.0 %fusion.29 = f32[8,128,2,2,128]{4,1,3,0,2:T(8,128)S(1)} fusion(f32[2,2,128,128,1]{3,2,1,4,0:T(8,128)S(1)} %copy-done.7, f32[8,128,128]{2,1,0:T(8,128)} %collective-permute-done, f32[2,8,128,128]{3,2,1,0:T(8,128)S(1)} %bitcast.248, s32[]{:T(128)S(6)} %select_n.90), kind=kOutput, calls=%fused_computation.58 | convolution fusion | flops 402784256 | bytes 3407876 | tf_op jit(solution)/shard_map/zxj,pcjm->pczxm/dot_general | solution.py:104
  60.9 1.4 copy.33
  62.3 6.2 %all-to-all-start = ((f32[32,8,8,128]{3,2,1,0:T(8,128)}), f32[32,8,8,128]{3,2,1,0:T(8,128)}, u32[]{:S(2)}, u32[]{:S(2)}) async-start(f32[32,8,8,128]{3,2,1,0:T(8,128)} %bitcast.15), calls=%async_computation | async-start | bytes 2097152 | tf_op jit(solution)/shard_map/all_to_all | solution.py:109
  68.7 1.7 collective-permute-start.3
  70.4 1.6 convolution_bitcast_fusion.1
  72.0 13.8 %collective-permute-done.3 = f32[4,128,128]{2,1,0:T(8,128)S(1)} collective-permute-done((f32[4,128,128]{2,1,0:T(8,128)S(1)}, f32[4,128,128]{2,1,0:T(8,128)S(1)}, u32[]{:S(2)}, u32[]{:S(2)}) %collective-permute-start.3) | collective-permute-done | bytes 262176 | tf_op jit(solution)/shard_map/ppermute | solution.py:56
  85.9 1.3 collective-permute-start.4
  87.8 4.9 %collective-permute-done.4 = f32[2,128,128]{2,1,0:T(8,128)S(1)} collective-permute-done((f32[2,128,128]{2,1,0:T(8,128)S(1)}, f32[2,128,128]{2,1,0:T(8,128)S(1)}, u32[]{:S(2)}, u32[]{:S(2)}) %collective-permute-start.4) | collective-permute-done | bytes 131104 | tf_op jit(solution)/shard_map/ppermute | solution.py:56
  93.3 2.5 %collective-permute-start.5 = (f32[1,128,128]{2,1,0:T(8,128)}, f32[1,128,128]{2,1,0:T(8,128)}, u32[]{:S(2)}, u32[]{:S(2)}) collective-permute-start(f32[1,128,128]{2,1,0:T(8,128)} %constant_dynamic-slice_fusion), channel_id=1, source_target_pairs={{0,16},{2,18},{4,20},{6,22},{8,24},{10,26},{12,28},{14,30},{16,0},... | collective-permute-start | bytes 196616 | tf_op jit(solution)/shard_map/ppermute | solution.py:56
  95.8 2.4 %copy.72 = f32[32,8,8,128]{3,1,2,0:T(8,128)} copy(f32[32,8,8,128]{3,2,1,0:T(8,128)} %bitcast.80) | data formatting | bytes 2097152
  98.2 2.5 %copy.35 = f32[1024,256]{1,0:T(8,128)} copy(f32[1024,256]{0,1:T(8,128)} %bitcast.252) | data formatting | bytes 2097152 | tf_op jit(solution)/shard_map/dot_general | solution.py:110
  100.8 2.9 %fusion.50 = f32[16,16,8,128]{3,1,2,0:T(8,128)} fusion(f32[16,16,256,1]{2,1,3,0:T(8,128)} %constant.184, f32[8,128,256,1]{2,1,0,3:T(8,128)} %bitcast.251), kind=kOutput, calls=%fused_computation.118 | convolution fusion | flops 402653184 | bytes 2359296 | tf_op jit(solution)/shard_map/dot_general | solution.py:110
  103.7 4.3 %all-to-all-start.2 = ((f32[16,16,8,128]{3,1,2,0:T(8,128)}), f32[16,16,8,128]{3,1,2,0:T(8,128)}, u32[]{:S(2)}, u32[]{:S(2)}) async-start(f32[16,16,8,128]{3,1,2,0:T(8,128)} %fusion.50), calls=%async_computation.2 | async-start | bytes 2097152 | tf_op jit(solution)/shard_map/all_to_all | solution.py:111
  108.0 1.3 pad_maximum_fusion.1
  109.3 1.5 multiply_bitcast_fusion
  110.9 2.0 %convolution_bitcast_fusion.2 = f32[32,8,8,128]{3,1,2,0:T(8,128)S(1)} fusion(f32[256,256]{1,0:T(8,128)} %constant.168.clone, f32[32,8,8,128]{3,2,1,0:T(8,128)} %all-to-all-done), kind=kOutput, calls=%fused_computation.16 | convolution fusion | flops 402653184 | bytes 2359296 | tf_op jit(solution)/shard_map/dot_general | solution.py:118
  113.9 0.8 copy-done.5
  114.8 2.5 %fusion.17 = (f32[256,1024]{1,0:T(8,128)S(1)}, f32[1024]{0:T(1024)S(1)}) fusion(f32[32,8,8,128]{3,2,1,0:T(8,128)S(1)} %bitcast.255, f32[256]{0:T(256)S(1)} %copy-done.17, f32[1024]{0:T(1024)S(1)} %bitcast_add_fusion.7, f32[32,8,8,128]{3,2,1,0:T(8,128)S(1)} %bitcast.256, f32[256,256]{1,0:T(8,128)S(1)} %copy-done.16, f32[32,8,8,128]{3,2,1,0:T(8,128)} %all-to-all-done), kind=kOutput, calls=%fused_computation.28 | convolution fusion | flops 406060032 | bytes 4465664 | tf_op jit(solution)/shard_map/dot_general | solution.py:115
  117.7 13.2 %all-to-all-done.2 = f32[16,16,8,128]{3,1,2,0:T(8,128)} async-done(((f32[16,16,8,128]{3,1,2,0:T(8,128)}), f32[16,16,8,128]{3,1,2,0:T(8,128)}, u32[]{:S(2)}, u32[]{:S(2)}) %all-to-all-start.2) | async-done | bytes 1048608 | tf_op jit(solution)/shard_map/all_to_all | solution.py:111
  130.9 3.3 %fusion.25 = (f32[16,128,128]{2,1,0:T(8,128)S(1)}, f32[16,128,128]{2,1,0:T(8,128)S(1)}) fusion(f32[1,16,128,128]{3,2,1,0:T(8,128)S(1)} %copy-done, f32[16,16,8,128]{3,0,2,1:T(8,128)} %bitcast.33, f32[16,128,128]{2,1,0:T(8,128)S(1)} %copy-done.3, f32[128,128,1]{1,0,2:T(8,128)S(1)} %copy-done.10), kind=kOutput, calls=%fused_computation.54 | convolution fusion | flops 204472320 | bytes 5308416 | tf_op jit(solution)/shard_map/zxk,ik->zxi/dot_general | solution.py:149
  134.2 3.0 %multiply_reduce_fusion = (f32[128]{0:T(128)S(1)}, f32[128]{0:T(128)S(1)}, f32[128]{0:T(128)S(1)}, f32[128]{0:T(128)S(1)}, f32[128]{0:T(128)S(1)}, /*index=5*/f32[128]{0:T(128)S(1)}, f32[1,16,128,128]{3,2,1,0:T(8,128)}) fusion(f32[16,128,128]{2,1,0:T(8,128)S(1)} %get-tuple-element.40, f32[16,128,128]{2,1,0:T(8,128)S(1)} %get-tuple-element.39, ...), kind=kLoop, calls=%fused_computation.47 | loop fusion | flops 5242112 | bytes 5245952 | tf_op jit(solution)/shard_map/reduce_sum | solution.py:156
  137.3 41.9 %psum.7 = f32[6,128]{1,0:T(8,128)S(1)} all-reduce(f32[6,128]{1,0:T(8,128)S(1)} %stack.2), channel_id=1, replica_groups=mesh['band'=16,'spin'=2] {'band','spin'}, use_global_device_ids=true, to_apply=%region_23.24 | all-reduce | flops 768 | bytes 6144 | tf_op jit(solution)/shard_map/psum | solution.py:168
  (69 shorter events, 6.4 us)
Async XLA Ops:
  2.9 59.3 %all-to-all-start.1 = ((f32[16,16,8,128]{3,2,1,0:T(8,128)}), f32[16,16,8,128]{3,2,1,0:T(8,128)}, u32[]{:S(2)}, u32[]{:S(2)}) async-start(f32[16,16,8,128]{3,2,1,0:T(8,128)} %copy_bitcast_fusion), calls=%async_computation.1 | async-start | bytes 2097152 | tf_op jit(solution)/shard_map/all_to_all | solution.py:78
  10.4 6.6 %copy-start.15 = (s32[1,2]{1,0:T(1,128)S(1)}, s32[1,2]{1,0:T(1,128)}, u32[]{:S(2)}) copy-start(s32[1,2]{1,0:T(1,128)} %param.17) | copy-start | bytes 28
  40.5 1.6 copy-start
  40.6 3.9 %copy-start.13 = (f32[128]{0:T(128)S(1)}, f32[128]{0:T(128)}, u32[]{:S(2)}) copy-start(f32[128]{0:T(128)} %constant.170.clone) | copy-start | bytes 1540
  40.6 4.2 %copy-start.8 = (s32[3,16384]{1,0:T(4,128)S(1)}, s32[3,16384]{1,0:T(4,128)}, u32[]{:S(2)}) copy-start(s32[3,16384]{1,0:T(4,128)} %param.18) | copy-start | bytes 589828
  41.6 3.9 %collective-permute-start.1 = (f32[8,2,128,128]{3,2,1,0:T(8,128)}, f32[8,2,128,128]{3,2,1,0:T(8,128)}, u32[]{:S(2)}, u32[]{:S(2)}) collective-permute-start(f32[8,2,128,128]{3,2,1,0:T(8,128)} %dynamic-slice_bitcast_fusion.2), channel_id=1, source_target_pairs={{0,2},{2,0},{4,6},{6,4},{8,10},{10,8},{12,14},{14,12},{16,18},{18,... | collective-permute-start | bytes 3145736 | tf_op jit(solution)/shard_map/ppermute | solution.py:56
  43.0 15.1 %collective-permute-start = (f32[8,128,128]{2,1,0:T(8,128)}, f32[8,128,128]{2,1,0:T(8,128)}, u32[]{:S(2)}, u32[]{:S(2)}) collective-permute-start(f32[8,128,128]{2,1,0:T(8,128)} %dynamic-slice_bitcast_fusion.4), channel_id=1, source_target_pairs={{0,1},{1,0},{2,3},{3,2},{4,5},{5,4},{6,7},{7,6},{8,9},{9,8},{10,11... | collective-permute-start | bytes 1572872 | tf_op jit(solution)/shard_map/ppermute | solution.py:81
  45.6 12.6 %copy-start.7 = (f32[2,2,128,128,1]{3,2,1,4,0:T(8,128)S(1)}, f32[2,2,128,128,1]{3,2,1,4,0:T(8,128)}, u32[]{:S(2)}) copy-start(f32[2,2,128,128,1]{3,2,1,4,0:T(8,128)} %constant.181) | copy-start | bytes 786436
  47.0 1.4 copy-start.1
  47.0 13.2 %copy-start.9 = (f32[2,16,8,128,1,1]{3,1,0,2,5,4:T(8,128)S(1)}, f32[2,16,8,128,1,1]{3,1,0,2,5,4:T(8,128)}, u32[]{:S(2)}) copy-start(f32[2,16,8,128,1,1]{3,1,0,2,5,4:T(8,128)} %constant.182) | copy-start | bytes 393220
  47.8 20.8 %collective-permute-start.2 = (f32[8,128,128]{2,1,0:T(8,128)}, f32[8,128,128]{2,1,0:T(8,128)S(1)}, u32[]{:S(2)}, u32[]{:S(2)}) collective-permute-start(f32[8,128,128]{2,1,0:T(8,128)} %dynamic-slice_bitcast_fusion.3), channel_id=1, source_target_pairs={{0,1},{1,0},{2,3},{3,2},{4,5},{5,4},{6,7},{7,6},{8,9},{9,8},{10,11... | collective-permute-start | bytes 1572872 | tf_op jit(solution)/shard_map/ppermute | solution.py:61
  60.9 7.6 %copy-start.6 = (f32[1,3,128,128]{3,1,2,0:T(4,128)S(1)}, f32[1,3,128,128]{3,1,2,0:T(4,128)}, u32[]{:S(2)}) copy-start(f32[1,3,128,128]{3,1,2,0:T(4,128)} %convert_bitcast_fusion) | copy-start | bytes 589828
  60.9 7.6 %copy-start.14 = (f32[3]{0:T(128)S(1)}, f32[3]{0:T(128)}, u32[]{:S(2)}) copy-start(f32[3]{0:T(128)} %constant.172.clone) | copy-start | bytes 40
  60.9 7.7 %copy-start.2 = (f32[8,2,128,128]{3,2,1,0:T(8,128)S(1)}, f32[8,2,128,128]{3,2,1,0:T(8,128)}, u32[]{:S(2)}) copy-start(f32[8,2,128,128]{3,2,1,0:T(8,128)} %copy-done.1) | copy-start | bytes 3145732
  62.3 8.2 %copy-start.10 = (f32[128,128,1]{1,0,2:T(8,128)S(1)}, f32[128,128,1]{1,0,2:T(8,128)}, u32[]{:S(2)}) copy-start(f32[128,128,1]{1,0,2:T(8,128)} %constant.183) | copy-start | bytes 196612
  62.3 41.4 %all-to-all-start = ((f32[32,8,8,128]{3,2,1,0:T(8,128)}), f32[32,8,8,128]{3,2,1,0:T(8,128)}, u32[]{:S(2)}, u32[]{:S(2)}) async-start(f32[32,8,8,128]{3,2,1,0:T(8,128)} %bitcast.15), calls=%async_computation | async-start | bytes 2097152 | tf_op jit(solution)/shard_map/all_to_all | solution.py:109
  68.7 18.5 %copy-start.4 = (f32[2,256,8,128]{3,2,1,0:T(8,128)S(1)}, f32[2,256,8,128]{3,2,1,0:T(8,128)}, u32[]{:S(2)}) copy-start(f32[2,256,8,128]{3,2,1,0:T(8,128)} %param.20) | copy-start | bytes 6291460
  68.7 17.1 %collective-permute-start.3 = (f32[4,128,128]{2,1,0:T(8,128)S(1)}, f32[4,128,128]{2,1,0:T(8,128)S(1)}, u32[]{:S(2)}, u32[]{:S(2)}) collective-permute-start(f32[4,128,128]{2,1,0:T(8,128)S(1)} %dynamic-slice_bitcast_fusion.5), channel_id=1, source_target_pairs={{0,4},{2,6},{4,0},{6,2},{8,12},{10,14},{12,8},{14,10},{16,20},{18,... | collective-permute-start | bytes 786440 | tf_op jit(solution)/shard_map/ppermute | solution.py:56
  85.9 6.8 %collective-permute-start.4 = (f32[2,128,128]{2,1,0:T(8,128)S(1)}, f32[2,128,128]{2,1,0:T(8,128)S(1)}, u32[]{:S(2)}, u32[]{:S(2)}) collective-permute-start(f32[2,128,128]{2,1,0:T(8,128)S(1)} %dynamic-slice_bitcast_fusion.6), channel_id=1, source_target_pairs={{0,8},{2,10},{4,12},{6,14},{8,0},{10,2},{12,4},{14,6},{16,24},{18,... | collective-permute-start | bytes 393224 | tf_op jit(solution)/shard_map/ppermute | solution.py:56
  93.3 16.0 %collective-permute-start.5 = (f32[1,128,128]{2,1,0:T(8,128)}, f32[1,128,128]{2,1,0:T(8,128)}, u32[]{:S(2)}, u32[]{:S(2)}) collective-permute-start(f32[1,128,128]{2,1,0:T(8,128)} %constant_dynamic-slice_fusion), channel_id=1, source_target_pairs={{0,16},{2,18},{4,20},{6,22},{8,24},{10,26},{12,28},{14,30},{16,0},... | collective-permute-start | bytes 196616 | tf_op jit(solution)/shard_map/ppermute | solution.py:56
  103.7 27.2 %all-to-all-start.2 = ((f32[16,16,8,128]{3,1,2,0:T(8,128)}), f32[16,16,8,128]{3,1,2,0:T(8,128)}, u32[]{:S(2)}, u32[]{:S(2)}) async-start(f32[16,16,8,128]{3,1,2,0:T(8,128)} %fusion.50), calls=%async_computation.2 | async-start | bytes 2097152 | tf_op jit(solution)/shard_map/all_to_all | solution.py:111
  113.5 1.2 copy-start.5
  113.5 1.3 copy-start.16
  113.5 1.2 copy-start.17
  114.8 2.6 %copy-start.11 = (f32[256]{0:T(256)S(1)}, f32[256]{0:T(256)}, u32[]{:S(2)}) copy-start(f32[256]{0:T(256)} %constant.179) | copy-start | bytes 3076
  114.8 2.6 %copy-start.12 = (f32[256]{0:T(256)S(1)}, f32[256]{0:T(256)}, u32[]{:S(2)}) copy-start(f32[256]{0:T(256)} %constant.180) | copy-start | bytes 3076
  114.8 16.1 %copy-start.3 = (f32[16,128,128]{2,1,0:T(8,128)S(1)}, f32[16,128,128]{2,1,0:T(8,128)}, u32[]{:S(2)}) copy-start(f32[16,128,128]{2,1,0:T(8,128)} %convolution_bitcast_fusion.1) | copy-start | bytes 3145732
where the time goes:
time: 181 us; the launch traced here: 180 us
  blocking collectives  41.9 us (23%)
  waiting for transfers between devices  41.7 us (23%)
  other arithmetic  40.1 us (22%)
  starting transfers between devices  25.8 us (14%)
  matrix products  15.1 us (8%)
  local copies, waits for them, and re-layouts  14.2 us (8%)
    psum x1, blocking collectives, shards(): stress = jnp.sum(lax.psum(lanewise, ('band', 'spin')), axis=1)  41.9 us
    reduce_sum x1, other arithmetic, shards(): jnp.sum((piece[0] * piece[0] + piece[1] * piece[1]) * weights[:, None], a...  23.5 us
    ppermute x4, waiting for transfers between devices, scatter_sum(): rest = keep + lax.ppermute(give, 'band', pair_up(band_devices, bit))  18.7 us
    all_to_all x1, waiting for transfers between devices, shards(): lax.all_to_all(gradz_col.reshape(band_devices, planes, rows, ny), 'band',...  13.2 us
    ppermute x1, waiting for transfers between devices, shards(): total = keep + lax.ppermute(give, 'spin', pair_up(spins, 1))  9.74 us
    all_to_all x1, starting transfers between devices, shards(): lax.all_to_all(dens_send, 'band', 0, 0, tiled=True).reshape(nz, rows * ny)  7.46 us
    convert_element_type x1, other arithmetic, shards(): piece = coefficients[0].astype(jnp.float32)  6.6 us
    all_to_all x1, starting transfers between devices, shards(): lax.all_to_all(plane, ('band', 'spin'), 0, 0, tiled=True)  6.16 us
  transfers between devices with their start and end apart: 9, of which 4 were waited for; matrix products, arithmetic and copies ran while one was open for 33% of the time, Pallas kernels for 0%

commit v1 on v0

--- a/solution.py
+++ b/solution.py
@@ -165,7 +165,7 @@
     kinetic_density = 0.5 * (gvec[0] ** 2 + gvec[1] ** 2 + gvec[2] ** 2) * kinetic_weight
     kinetic = six(kinetic_weight * (-1.0 / waves), gvec[0], gvec[1], gvec[2], 0)
     lanewise = jnp.stack([r + x + k for r, x, k in zip(recip, xc, kinetic)])
-    stress = jnp.sum(lax.psum(lanewise, ("band", "spin")), axis=1)
+    stress = jnp.sum(lax.all_gather(lanewise, axis_name=("band", "spin")).sum(axis=0), axis=1)
     return (stress, kinetic_density.reshape(chunk), square[None])
 
 

time: 181 us -> 209 us (1.15)
  blocking collectives: 41.9 us -> 69.9 us
    all_gather x0 -> x1, blocking collectives: none -> 69.9 us  [shards(): lax.all_gather(lanewise, axis_name=('band', 'spin')).sum(axis=0)]
    psum x1 -> x0, blocking collectives: 41.9 us -> none  [shards(): stress = jnp.sum(lax.psum(lanewise, ('band', 'spin')), axis=1)]
  transfers between devices with their start and end apart: 9 -> 9, of which waited for: 4 -> 4; matrix products, arithmetic and copies ran while one was open for 33% -> 28% of each run, Pallas kernels for 0% -> 0%
where the time goes in v1:
time: 209 us; the launch traced here: 208 us
  blocking collectives  69.9 us (33%)
  waiting for transfers between devices  41.7 us (20%)
  other arithmetic  40.1 us (19%)
  starting transfers between devices  25.8 us (12%)
  matrix products  15.1 us (7%)
  local copies, waits for them, and re-layouts  14.2 us (7%)
    all_gather x1, blocking collectives, shards(): lax.all_gather(lanewise, axis_name=('band', 'spin')).sum(axis=0)  69.9 us
    reduce_sum x1, other arithmetic, shards(): jnp.sum((piece[0] * piece[0] + piece[1] * piece[1]) * weights[:, None], a...  23.5 us
    ppermute x4, waiting for transfers between devices, scatter_sum(): rest = keep + lax.ppermute(give, 'band', pair_up(band_devices, bit))  18.7 us
    all_to_all x1, waiting for transfers between devices, shards(): lax.all_to_all(gradz_col.reshape(band_devices, planes, rows, ny), 'band',...  13.2 us
    ppermute x1, waiting for transfers between devices, shards(): total = keep + lax.ppermute(give, 'spin', pair_up(spins, 1))  9.74 us
    all_to_all x1, starting transfers between devices, shards(): lax.all_to_all(dens_send, 'band', 0, 0, tiled=True).reshape(nz, rows * ny)  7.46 us
    convert_element_type x1, other arithmetic, shards(): piece = coefficients[0].astype(jnp.float32)  6.6 us
    all_to_all x1, starting transfers between devices, shards(): lax.all_to_all(plane, ('band', 'spin'), 0, 0, tiled=True)  6.16 us
  transfers between devices with their start and end apart: 9, of which 4 were waited for; matrix products, arithmetic and copies ran while one was open for 28% of the time, Pallas kernels for 0%

profile of v1, /device:TPU:0, one launch (start us, length us, event | category | flops | bytes accessed | tf_op | source)
XLA Modules:
  0.0 207.8 jit_solution(2746708768028299003)
XLA Ops:
  0.6 2.3 %copy_bitcast_fusion = f32[16,16,8,128]{3,2,1,0:T(8,128)} fusion(f32[1,16,128,128]{3,2,1,0:T(8,128)} %param.19), kind=kLoop, calls=%fused_computation.46 | loop fusion | bytes 2097152 | tf_op jit(solution)/shard_map/transpose | solution.py:77
  2.9 7.5 %all-to-all-start.1 = ((f32[16,16,8,128]{3,2,1,0:T(8,128)}), f32[16,16,8,128]{3,2,1,0:T(8,128)}, u32[]{:S(2)}, u32[]{:S(2)}) async-start(f32[16,16,8,128]{3,2,1,0:T(8,128)} %copy_bitcast_fusion), calls=%async_computation.1 | async-start | bytes 2097152 | tf_op jit(solution)/shard_map/all_to_all | solution.py:78
  10.4 6.6 %convert_element_type.18 = f32[1,2,2,524288]{3,2,1,0:T(2,128)} convert(bf16[1,2,2,524288]{3,2,1,0:T(2,128)(2,1)} %param.16) | non-fusion elementwise | flops 2097152 | bytes 12582912 | tf_op jit(solution)/shard_map/convert_element_type | solution.py:83
  17.1 23.5 %fusion.3 = f32[524288]{0:T(1024)S(1)} fusion(f32[1,2,2,524288]{3,2,1,0:T(2,128)} %convert_element_type.18, f32[2]{0:T(128)S(1)} %multiply_bitcast_fusion.1), kind=kLoop, calls=%fused_computation.5 | loop fusion | flops 4718592 | bytes 10485768 | tf_op jit(solution)/shard_map/reduce_sum | solution.py:84
  40.6 1.0 dynamic-slice_bitcast_fusion.2
  42.2 0.9 dynamic-slice_bitcast_fusion.4
  43.0 1.5 collective-permute-start
  45.6 1.4 bitcast_add_fusion
  47.0 0.8 dynamic-slice_bitcast_fusion.3
  48.4 9.7 %collective-permute-done = f32[8,128,128]{2,1,0:T(8,128)} collective-permute-done((f32[8,128,128]{2,1,0:T(8,128)}, f32[8,128,128]{2,1,0:T(8,128)}, u32[]{:S(2)}, u32[]{:S(2)}) %collective-permute-start) | collective-permute-done | bytes 524320 | tf_op jit(solution)/shard_map/ppermute | solution.py:81
  58.1 2.0 fusion.29
  60.9 1.4 copy.37
  62.3 6.2 %all-to-all-start = ((f32[32,8,8,128]{3,2,1,0:T(8,128)}), f32[32,8,8,128]{3,2,1,0:T(8,128)}, u32[]{:S(2)}, u32[]{:S(2)}) async-start(f32[32,8,8,128]{3,2,1,0:T(8,128)} %bitcast.15), calls=%async_computation | async-start | bytes 2097152 | tf_op jit(solution)/shard_map/all_to_all | solution.py:109
  68.7 1.7 collective-permute-start.3
  70.4 1.6 convolution_bitcast_fusion.1
  72.0 13.8 %collective-permute-done.3 = f32[4,128,128]{2,1,0:T(8,128)S(1)} collective-permute-done((f32[4,128,128]{2,1,0:T(8,128)S(1)}, f32[4,128,128]{2,1,0:T(8,128)S(1)}, u32[]{:S(2)}, u32[]{:S(2)}) %collective-permute-start.3) | collective-permute-done | bytes 262176 | tf_op jit(solution)/shard_map/ppermute | solution.py:56
  85.9 1.3 collective-permute-start.4
  87.8 4.9 %collective-permute-done.4 = f32[2,128,128]{2,1,0:T(8,128)S(1)} collective-permute-done((f32[2,128,128]{2,1,0:T(8,128)S(1)}, f32[2,128,128]{2,1,0:T(8,128)S(1)}, u32[]{:S(2)}, u32[]{:S(2)}) %collective-permute-start.4) | collective-permute-done | bytes 131104 | tf_op jit(solution)/shard_map/ppermute | solution.py:56
  93.3 2.5 %collective-permute-start.5 = (f32[1,128,128]{2,1,0:T(8,128)}, f32[1,128,128]{2,1,0:T(8,128)}, u32[]{:S(2)}, u32[]{:S(2)}) collective-permute-start(f32[1,128,128]{2,1,0:T(8,128)} %constant_dynamic-slice_fusion), channel_id=1, source_target_pairs={{0,16},{2,18},{4,20},{6,22},{8,24},{10,26},{12,28},{14,30},{16,0},... | collective-permute-start | bytes 196616 | tf_op jit(solution)/shard_map/ppermute | solution.py:56
  95.8 2.4 %copy.76 = f32[32,8,8,128]{3,1,2,0:T(8,128)} copy(f32[32,8,8,128]{3,2,1,0:T(8,128)} %bitcast.81) | data formatting | bytes 2097152
  98.2 2.5 %copy.39 = f32[1024,256]{1,0:T(8,128)} copy(f32[1024,256]{0,1:T(8,128)} %bitcast.253) | data formatting | bytes 2097152 | tf_op jit(solution)/shard_map/dot_general | solution.py:110
  100.8 2.9 %fusion.50 = f32[16,16,8,128]{3,1,2,0:T(8,128)} fusion(f32[16,16,256,1]{2,1,3,0:T(8,128)} %constant.184, f32[8,128,256,1]{2,1,0,3:T(8,128)} %bitcast.252), kind=kOutput, calls=%fused_computation.118 | convolution fusion | flops 402653184 | bytes 2359296 | tf_op jit(solution)/shard_map/dot_general | solution.py:110
  103.7 4.3 %all-to-all-start.2 = ((f32[16,16,8,128]{3,1,2,0:T(8,128)}), f32[16,16,8,128]{3,1,2,0:T(8,128)}, u32[]{:S(2)}, u32[]{:S(2)}) async-start(f32[16,16,8,128]{3,1,2,0:T(8,128)} %fusion.50), calls=%async_computation.2 | async-start | bytes 2097152 | tf_op jit(solution)/shard_map/all_to_all | solution.py:111
  108.0 1.3 pad_maximum_fusion.1
  109.3 1.5 multiply_bitcast_fusion
  110.9 2.0 convolution_bitcast_fusion.2
  113.9 0.8 copy-done.5
  114.8 2.5 %fusion.17 = (f32[256,1024]{1,0:T(8,128)S(1)}, f32[1024]{0:T(1024)S(1)}) fusion(f32[32,8,8,128]{3,2,1,0:T(8,128)S(1)} %bitcast.256, f32[256]{0:T(256)S(1)} %copy-done.17, f32[1024]{0:T(1024)S(1)} %bitcast_add_fusion.7, f32[32,8,8,128]{3,2,1,0:T(8,128)S(1)} %bitcast.257, f32[256,256]{1,0:T(8,128)S(1)} %copy-done.16, f32[32,8,8,128]{3,2,1,0:T(8,128)} %all-to-all-done), kind=kOutput, calls=%fused_computation.28 | convolution fusion | flops 406060032 | bytes 4465664 | tf_op jit(solution)/shard_map/dot_general | solution.py:115
  117.7 13.2 %all-to-all-done.2 = f32[16,16,8,128]{3,1,2,0:T(8,128)} async-done(((f32[16,16,8,128]{3,1,2,0:T(8,128)}), f32[16,16,8,128]{3,1,2,0:T(8,128)}, u32[]{:S(2)}, u32[]{:S(2)}) %all-to-all-start.2) | async-done | bytes 1048608 | tf_op jit(solution)/shard_map/all_to_all | solution.py:111
  130.9 3.3 %fusion.25 = (f32[16,128,128]{2,1,0:T(8,128)S(1)}, f32[16,128,128]{2,1,0:T(8,128)S(1)}) fusion(f32[1,16,128,128]{3,2,1,0:T(8,128)S(1)} %copy-done, f32[16,16,8,128]{3,0,2,1:T(8,128)} %bitcast.33, f32[16,128,128]{2,1,0:T(8,128)S(1)} %copy-done.3, f32[128,128,1]{1,0,2:T(8,128)S(1)} %copy-done.10), kind=kOutput, calls=%fused_computation.54 | convolution fusion | flops 204472320 | bytes 5308416 | tf_op jit(solution)/shard_map/zxk,ik->zxi/dot_general | solution.py:149
  134.2 3.0 %multiply_reduce_fusion = (f32[128]{0:T(128)S(1)}, f32[128]{0:T(128)S(1)}, f32[128]{0:T(128)S(1)}, f32[128]{0:T(128)S(1)}, f32[128]{0:T(128)S(1)}, /*index=5*/f32[128]{0:T(128)S(1)}, f32[1,16,128,128]{3,2,1,0:T(8,128)}) fusion(f32[16,128,128]{2,1,0:T(8,128)S(1)} %get-tuple-element.40, f32[16,128,128]{2,1,0:T(8,128)S(1)} %get-tuple-element.39, ...), kind=kLoop, calls=%fused_computation.47 | loop fusion | flops 5242112 | bytes 5245952 | tf_op jit(solution)/shard_map/reduce_sum | solution.py:156
  137.3 69.9 %all-gather.1 = f32[32,6,128]{2,1,0:T(8,128)S(1)} all-gather(f32[1,6,128]{2,1,0:T(8,128)S(1)} %bitcast.260), channel_id=2, replica_groups=mesh['band'=16,'spin'=2] {'band','spin'}, dimensions={0}, use_global_device_ids=true | all-gather | bytes 101376 | tf_op jit(solution)/shard_map/all_gather | solution.py:168
  (69 shorter events, 6.5 us)
Async XLA Ops:
  2.9 59.3 %all-to-all-start.1 = ((f32[16,16,8,128]{3,2,1,0:T(8,128)}), f32[16,16,8,128]{3,2,1,0:T(8,128)}, u32[]{:S(2)}, u32[]{:S(2)}) async-start(f32[16,16,8,128]{3,2,1,0:T(8,128)} %copy_bitcast_fusion), calls=%async_computation.1 | async-start | bytes 2097152 | tf_op jit(solution)/shard_map/all_to_all | solution.py:78
  10.4 6.6 %copy-start.15 = (s32[1,2]{1,0:T(1,128)S(1)}, s32[1,2]{1,0:T(1,128)}, u32[]{:S(2)}) copy-start(s32[1,2]{1,0:T(1,128)} %param.17) | copy-start | bytes 28
  40.5 1.6 copy-start
  40.6 3.9 %copy-start.13 = (f32[128]{0:T(128)S(1)}, f32[128]{0:T(128)}, u32[]{:S(2)}) copy-start(f32[128]{0:T(128)} %constant.170.clone) | copy-start | bytes 1540
  40.6 4.2 %copy-start.8 = (s32[3,16384]{1,0:T(4,128)S(1)}, s32[3,16384]{1,0:T(4,128)}, u32[]{:S(2)}) copy-start(s32[3,16384]{1,0:T(4,128)} %param.18) | copy-start | bytes 589828
  41.6 3.9 %collective-permute-start.1 = (f32[8,2,128,128]{3,2,1,0:T(8,128)}, f32[8,2,128,128]{3,2,1,0:T(8,128)}, u32[]{:S(2)}, u32[]{:S(2)}) collective-permute-start(f32[8,2,128,128]{3,2,1,0:T(8,128)} %dynamic-slice_bitcast_fusion.2), channel_id=1, source_target_pairs={{0,2},{2,0},{4,6},{6,4},{8,10},{10,8},{12,14},{14,12},{16,18},{18,... | collective-permute-start | bytes 3145736 | tf_op jit(solution)/shard_map/ppermute | solution.py:56
  43.0 15.1 %collective-permute-start = (f32[8,128,128]{2,1,0:T(8,128)}, f32[8,128,128]{2,1,0:T(8,128)}, u32[]{:S(2)}, u32[]{:S(2)}) collective-permute-start(f32[8,128,128]{2,1,0:T(8,128)} %dynamic-slice_bitcast_fusion.4), channel_id=1, source_target_pairs={{0,1},{1,0},{2,3},{3,2},{4,5},{5,4},{6,7},{7,6},{8,9},{9,8},{10,11... | collective-permute-start | bytes 1572872 | tf_op jit(solution)/shard_map/ppermute | solution.py:81
  45.6 12.6 %copy-start.7 = (f32[2,2,128,128,1]{3,2,1,4,0:T(8,128)S(1)}, f32[2,2,128,128,1]{3,2,1,4,0:T(8,128)}, u32[]{:S(2)}) copy-start(f32[2,2,128,128,1]{3,2,1,4,0:T(8,128)} %constant.181) | copy-start | bytes 786436
  47.0 1.4 copy-start.1
  47.0 13.2 %copy-start.9 = (f32[2,16,8,128,1,1]{3,1,0,2,5,4:T(8,128)S(1)}, f32[2,16,8,128,1,1]{3,1,0,2,5,4:T(8,128)}, u32[]{:S(2)}) copy-start(f32[2,16,8,128,1,1]{3,1,0,2,5,4:T(8,128)} %constant.182) | copy-start | bytes 393220
  47.8 20.8 %collective-permute-start.2 = (f32[8,128,128]{2,1,0:T(8,128)}, f32[8,128,128]{2,1,0:T(8,128)S(1)}, u32[]{:S(2)}, u32[]{:S(2)}) collective-permute-start(f32[8,128,128]{2,1,0:T(8,128)} %dynamic-slice_bitcast_fusion.3), channel_id=1, source_target_pairs={{0,1},{1,0},{2,3},{3,2},{4,5},{5,4},{6,7},{7,6},{8,9},{9,8},{10,11... | collective-permute-start | bytes 1572872 | tf_op jit(solution)/shard_map/ppermute | solution.py:61
  60.9 7.6 %copy-start.6 = (f32[1,3,128,128]{3,1,2,0:T(4,128)S(1)}, f32[1,3,128,128]{3,1,2,0:T(4,128)}, u32[]{:S(2)}) copy-start(f32[1,3,128,128]{3,1,2,0:T(4,128)} %convert_bitcast_fusion) | copy-start | bytes 589828
  60.9 7.6 %copy-start.14 = (f32[3]{0:T(128)S(1)}, f32[3]{0:T(128)}, u32[]{:S(2)}) copy-start(f32[3]{0:T(128)} %constant.172.clone) | copy-start | bytes 40
  60.9 7.7 %copy-start.2 = (f32[8,2,128,128]{3,2,1,0:T(8,128)S(1)}, f32[8,2,128,128]{3,2,1,0:T(8,128)}, u32[]{:S(2)}) copy-start(f32[8,2,128,128]{3,2,1,0:T(8,128)} %copy-done.1) | copy-start | bytes 3145732
  62.3 8.2 %copy-start.10 = (f32[128,128,1]{1,0,2:T(8,128)S(1)}, f32[128,128,1]{1,0,2:T(8,128)}, u32[]{:S(2)}) copy-start(f32[128,128,1]{1,0,2:T(8,128)} %constant.183) | copy-start | bytes 196612
  62.3 41.4 %all-to-all-start = ((f32[32,8,8,128]{3,2,1,0:T(8,128)}), f32[32,8,8,128]{3,2,1,0:T(8,128)}, u32[]{:S(2)}, u32[]{:S(2)}) async-start(f32[32,8,8,128]{3,2,1,0:T(8,128)} %bitcast.15), calls=%async_computation | async-start | bytes 2097152 | tf_op jit(solution)/shard_map/all_to_all | solution.py:109
  68.7 18.5 %copy-start.4 = (f32[2,256,8,128]{3,2,1,0:T(8,128)S(1)}, f32[2,256,8,128]{3,2,1,0:T(8,128)}, u32[]{:S(2)}) copy-start(f32[2,256,8,128]{3,2,1,0:T(8,128)} %param.20) | copy-start | bytes 6291460
  68.7 17.1 %collective-permute-start.3 = (f32[4,128,128]{2,1,0:T(8,128)S(1)}, f32[4,128,128]{2,1,0:T(8,128)S(1)}, u32[]{:S(2)}, u32[]{:S(2)}) collective-permute-start(f32[4,128,128]{2,1,0:T(8,128)S(1)} %dynamic-slice_bitcast_fusion.5), channel_id=1, source_target_pairs={{0,4},{2,6},{4,0},{6,2},{8,12},{10,14},{12,8},{14,10},{16,20},{18,... | collective-permute-start | bytes 786440 | tf_op jit(solution)/shard_map/ppermute | solution.py:56
  85.9 6.8 %collective-permute-start.4 = (f32[2,128,128]{2,1,0:T(8,128)S(1)}, f32[2,128,128]{2,1,0:T(8,128)S(1)}, u32[]{:S(2)}, u32[]{:S(2)}) collective-permute-start(f32[2,128,128]{2,1,0:T(8,128)S(1)} %dynamic-slice_bitcast_fusion.6), channel_id=1, source_target_pairs={{0,8},{2,10},{4,12},{6,14},{8,0},{10,2},{12,4},{14,6},{16,24},{18,... | collective-permute-start | bytes 393224 | tf_op jit(solution)/shard_map/ppermute | solution.py:56
  93.3 16.0 %collective-permute-start.5 = (f32[1,128,128]{2,1,0:T(8,128)}, f32[1,128,128]{2,1,0:T(8,128)}, u32[]{:S(2)}, u32[]{:S(2)}) collective-permute-start(f32[1,128,128]{2,1,0:T(8,128)} %constant_dynamic-slice_fusion), channel_id=1, source_target_pairs={{0,16},{2,18},{4,20},{6,22},{8,24},{10,26},{12,28},{14,30},{16,0},... | collective-permute-start | bytes 196616 | tf_op jit(solution)/shard_map/ppermute | solution.py:56
  103.7 27.2 %all-to-all-start.2 = ((f32[16,16,8,128]{3,1,2,0:T(8,128)}), f32[16,16,8,128]{3,1,2,0:T(8,128)}, u32[]{:S(2)}, u32[]{:S(2)}) async-start(f32[16,16,8,128]{3,1,2,0:T(8,128)} %fusion.50), calls=%async_computation.2 | async-start | bytes 2097152 | tf_op jit(solution)/shard_map/all_to_all | solution.py:111
  113.5 1.2 copy-start.5
  113.5 1.3 copy-start.16
  113.5 1.2 copy-start.17
  114.8 2.6 %copy-start.11 = (f32[256]{0:T(256)S(1)}, f32[256]{0:T(256)}, u32[]{:S(2)}) copy-start(f32[256]{0:T(256)} %constant.179) | copy-start | bytes 3076
  114.8 2.6 %copy-start.12 = (f32[256]{0:T(256)S(1)}, f32[256]{0:T(256)}, u32[]{:S(2)}) copy-start(f32[256]{0:T(256)} %constant.180) | copy-start | bytes 3076
  114.8 16.1 %copy-start.3 = (f32[16,128,128]{2,1,0:T(8,128)S(1)}, f32[16,128,128]{2,1,0:T(8,128)}, u32[]{:S(2)}) copy-start(f32[16,128,128]{2,1,0:T(8,128)} %convolution_bitcast_fusion.1) | copy-start | bytes 3145732
